TPU v7x, 32 devices: a whole 2x2x4 slice. The times are simulated.
32 devices in a mesh: dom: 8 (over z, y), sub: 4 (over x, core).
Axes of the slice: x: 2, y: 2, z: 4, core: 2. Of those that a mesh axis runs over, the one named last changes fastest.
Arguments:
- node_state: bfloat16 [64, 32768], P(None, ('dom', 'sub')), may hold values from -6 to 6
- edge_state: bfloat16 [64, 98304], P(None, ('dom', 'sub')), may hold values from -6 to 6
- senders: int32 [98304], P(('dom', 'sub')), may hold values from 0 to 2559, as said below
- receivers: int32 [98304], P(('dom', 'sub')), may hold values from 0 to 1023
- send_index: int32 [32, 12, 128], P(('dom', 'sub')), may hold values from -1 to 1023, as said below
- node_cotangent: bfloat16 [64, 32768], P(None, ('dom', 'sub')), may hold values from -6 to 6
- edge_cotangent: bfloat16 [64, 98304], P(None, ('dom', 'sub')), may hold values from -6 to 6
- edge_first: bfloat16 [192, 64], replicated, may hold values from -0.4375 to 0.4375
- edge_bias: float32 [64], replicated, may hold values from -3 to 3
- edge_second: bfloat16 [64, 64], replicated, may hold values from -0.75 to 0.75
- edge_gain: float32 [64], replicated, may hold values from 0.1 to 1.9
- edge_shift: float32 [64], replicated, may hold values from -3 to 3
- node_first: bfloat16 [128, 64], replicated, may hold values from -0.5 to 0.5
- node_bias: float32 [64], replicated, may hold values from -3 to 3
- node_second: bfloat16 [64, 64], replicated, may hold values from -0.75 to 0.75
- node_gain: float32 [64], replicated, may hold values from 0.1 to 1.9
Outputs:
- delta_state: bfloat16 [64, 32768], P(None, ('dom', 'sub'))
- delta_edges: bfloat16 [64, 98304], P(None, ('dom', 'sub'))
- delta_edgefirst: float32 [192, 64], replicated
- delta_edgebias: float32 [64], replicated
- delta_edgesecond: float32 [64, 64], replicated
- delta_edgegain: float32 [64], replicated
- delta_edgeshift: float32 [64], replicated
- delta_nodefirst: float32 [128, 64], replicated
- delta_nodebias: float32 [64], replicated
- delta_nodesecond: float32 [64, 64], replicated
- delta_nodegain: float32 [64], replicated
- delta_nodeshift: float32 [64], replicated
Inputs may be any that keep to these rules, and one draw needn't show every extreme that they name: `send_index`: block k = o * 4 + t of partition p = d * 4 + s lists own cells that p sends to the partition at dom index d + o - 1 and sub index t: live entries first, then -1. Blocks towards a dom index outside the mesh, and block 4 + s, hold only -1; every other block holds 32 to 128 live entries. Some partition receives a full block from every partition that sends to it. `senders`: an entry below 1024 is an own cell. An entry 1024 + k * 128 + j with k = o * 4 + u names ghost slot j of block k: the j-th entry of block o * 4 + s of the partition at dom index d + 1 - o and sub index u, and that entry is live.
All inputs are finite; a program needn't handle non-finite values.
Results may differ from a plain program's by a relative error of at most 0.0095.
Values may be sent and summed in bfloat16 or wider, within the bound.
A program may use at most 64 MiB of HBM per device.

v0:
```python
import math

import jax
import jax.numpy as jnp
from jax import lax
from jax.sharding import PartitionSpec as P

EPSILON = 1e-05


def from_behind(value, axis, steps):
    count = lax.axis_size(axis)
    first, last = (max(0, -steps), min(count, count - steps))
    return lax.ppermute(value, axis, [(source, source + steps) for source in range(first, last)])


def contract_first(first_operand, second_operand):
    return lax.dot_general(
        first_operand, second_operand, (((0,), (0,)), ((), ())), preferred_element_type=jnp.float32
    )


def contract_last(first_operand, second_operand):
    return lax.dot_general(
        first_operand, second_operand, (((1,), (1,)), ((), ())), preferred_element_type=jnp.float32
    )


def sigmoid_linear(values):
    return values * jax.nn.sigmoid(values)


def sigmoid_slope(values):
    logistic = jax.nn.sigmoid(values)
    return logistic * (1.0 + values * (1.0 - logistic))


def standardize(values):
    centered = values - jnp.mean(values, axis=0, keepdims=True)
    spread = lax.rsqrt(jnp.mean(centered * centered, axis=0, keepdims=True) + EPSILON)
    return (centered * spread, spread)


def normalize_back(upstream, scaled, spread, gain_vector):
    gain_delta = jnp.sum(upstream * scaled, axis=1)
    shift_delta = jnp.sum(upstream, axis=1)
    weighted = upstream * gain_vector[:, None]
    result = spread * (
        weighted
        - jnp.mean(weighted, axis=0, keepdims=True)
        - scaled * jnp.mean(weighted * scaled, axis=0, keepdims=True)
    )
    return (result, gain_delta, shift_delta)


def block_sizes(count, width):
    step = math.gcd(count, 512)
    piece = math.gcd(width, 2048)
    return (step, piece)


def pick_precision(values):
    if values.dtype == jnp.float32:
        return lax.Precision.HIGHEST
    return None


def column_gather(table, index):
    rows, width = table.shape
    count = index.shape[0]
    step, piece = block_sizes(count, width)
    blocks = index.reshape(count // step, step)
    precision = pick_precision(table)

    def one_block(number, result):
        chosen = lax.dynamic_index_in_dim(blocks, number, 0, keepdims=False)
        total = jnp.zeros((rows, step), jnp.float32)
        for begin in range(0, width, piece):
            columns = lax.iota(jnp.int32, piece) + begin
            selector = (columns[:, None] == chosen[None, :]).astype(table.dtype)
            total = total + jnp.dot(
                table[:, begin : begin + piece],
                selector,
                precision=precision,
                preferred_element_type=jnp.float32,
            )
        return lax.dynamic_update_slice_in_dim(result, total.astype(table.dtype), number * step, 1)

    return lax.fori_loop(0, count // step, one_block, jnp.zeros((rows, count), table.dtype))


def column_scatter(values, index, width):
    rows, count = values.shape
    step, piece = block_sizes(count, width)
    blocks = index.reshape(count // step, step)
    precision = pick_precision(values)

    def one_block(number, result):
        chosen = lax.dynamic_index_in_dim(blocks, number, 0, keepdims=False)
        portion = lax.dynamic_slice_in_dim(values, number * step, step, 1)
        pieces = []
        for begin in range(0, width, piece):
            columns = lax.iota(jnp.int32, piece) + begin
            selector = (chosen[:, None] == columns[None, :]).astype(values.dtype)
            pieces.append(
                jnp.dot(portion, selector, precision=precision, preferred_element_type=jnp.float32)
            )
        return result + jnp.concatenate(pieces, axis=1)

    return lax.fori_loop(0, count // step, one_block, jnp.zeros((rows, width), jnp.float32))


def local_backward(
    extended,
    node_state,
    edge_state,
    senders,
    receivers,
    node_cotangent,
    edge_cotangent,
    edge_first,
    edge_bias,
    edge_second,
    edge_gain,
    edge_shift,
    node_first,
    node_bias,
    node_second,
    node_gain,
):
    features, cell_count = node_state.shape
    sender_rows = column_gather(extended, senders)
    receiver_rows = column_gather(node_state, receivers)
    stacked = jnp.concatenate([sender_rows, receiver_rows, edge_state], axis=0)
    edge_linear = contract_first(edge_first, stacked) + edge_bias[:, None]
    edge_active = sigmoid_linear(edge_linear).astype(jnp.bfloat16)
    edge_output = contract_first(edge_second, edge_active)
    edge_scaled, edge_spread = standardize(edge_output)
    message = (edge_scaled * edge_gain[:, None] + edge_shift[:, None]).astype(jnp.bfloat16)
    summed = column_scatter(message, receivers, cell_count)
    node_input = jnp.concatenate([node_state, summed.astype(jnp.bfloat16)], axis=0)
    node_linear = contract_first(node_first, node_input) + node_bias[:, None]
    node_active = sigmoid_linear(node_linear).astype(jnp.bfloat16)
    node_output = contract_first(node_second, node_active)
    node_scaled, node_spread = standardize(node_output)
    upstream = node_cotangent.astype(jnp.float32)
    node_delta, nodegain_delta, nodeshift_delta = normalize_back(
        upstream, node_scaled, node_spread, node_gain
    )
    node_delta = node_delta.astype(jnp.bfloat16)
    nodesecond_delta = contract_last(node_active, node_delta)
    node_hidden = jnp.dot(
        node_second, node_delta, preferred_element_type=jnp.float32
    ) * sigmoid_slope(node_linear)
    nodebias_delta = jnp.sum(node_hidden, axis=1)
    node_hidden = node_hidden.astype(jnp.bfloat16)
    nodefirst_delta = contract_last(node_input, node_hidden)
    node_back = jnp.dot(node_first, node_hidden, preferred_element_type=jnp.float32)
    message_delta = edge_cotangent.astype(jnp.float32) + column_gather(
        node_back[features:], receivers
    )
    edge_delta, edgegain_delta, edgeshift_delta = normalize_back(
        message_delta, edge_scaled, edge_spread, edge_gain
    )
    edge_delta = edge_delta.astype(jnp.bfloat16)
    edgesecond_delta = contract_last(edge_active, edge_delta)
    edge_hidden = jnp.dot(
        edge_second, edge_delta, preferred_element_type=jnp.float32
    ) * sigmoid_slope(edge_linear)
    edgebias_delta = jnp.sum(edge_hidden, axis=1)
    edge_hidden = edge_hidden.astype(jnp.bfloat16)
    edgefirst_delta = contract_last(stacked, edge_hidden)
    edge_back = jnp.dot(edge_first, edge_hidden, preferred_element_type=jnp.float32)
    edge_result = (edge_cotangent.astype(jnp.float32) + edge_back[2 * features :]).astype(
        jnp.bfloat16
    )
    scattered = column_scatter(edge_back[:features], senders, extended.shape[1])
    local_delta = (
        scattered[:, :cell_count]
        + column_scatter(edge_back[features : 2 * features], receivers, cell_count)
        + node_back[:features]
        + upstream
    )
    ghost_delta = scattered[:, cell_count:]
    partials = (
        edgefirst_delta,
        edgebias_delta,
        edgesecond_delta,
        edgegain_delta,
        edgeshift_delta,
        nodefirst_delta,
        nodebias_delta,
        nodesecond_delta,
        nodegain_delta,
        nodeshift_delta,
    )
    return (local_delta, ghost_delta, edge_result, partials)


def on_device(
    node_state,
    edge_state,
    senders,
    receivers,
    send_index,
    node_cotangent,
    edge_cotangent,
    edge_first,
    edge_bias,
    edge_second,
    edge_gain,
    edge_shift,
    node_first,
    node_bias,
    node_second,
    node_gain,
):
    features, cell_count = node_state.shape
    sub_count = lax.axis_size("sub")
    peer_count = 3 * sub_count
    halo_width = send_index.shape[2]
    index_rows = send_index.reshape(peer_count, halo_width)
    live_slots = index_rows >= 0
    safe_index = jnp.where(live_slots, index_rows, 0).reshape(-1)
    picked = column_gather(node_state, safe_index).reshape(features, peer_count, halo_width)
    outgoing = jnp.where(live_slots[None], picked, jnp.zeros_like(picked))
    blocks = outgoing.reshape(features, 3, sub_count, halo_width)
    across = lax.all_to_all(blocks, "sub", split_axis=2, concat_axis=2, tiled=True)
    upper = from_behind(across[:, 0], "dom", -1)
    lower = from_behind(across[:, 2], "dom", 1)
    ghost_rows = jnp.stack([upper, across[:, 1], lower], axis=1).reshape(
        features, peer_count, halo_width
    )
    extended = jnp.concatenate([node_state, ghost_rows.reshape(features, -1)], axis=1)
    local_delta, ghost_delta, edge_result, partials = local_backward(
        extended,
        node_state,
        edge_state,
        senders,
        receivers,
        node_cotangent,
        edge_cotangent,
        edge_first,
        edge_bias,
        edge_second,
        edge_gain,
        edge_shift,
        node_first,
        node_bias,
        node_second,
        node_gain,
    )
    ghost_delta = ghost_delta.reshape(features, peer_count, halo_width)
    grouped = ghost_delta.reshape(features, 3, sub_count, halo_width)
    further = from_behind(grouped[:, 0].astype(jnp.bfloat16), "dom", 1).astype(jnp.float32)
    nearer = from_behind(grouped[:, 2].astype(jnp.bfloat16), "dom", -1).astype(jnp.float32)
    regrouped = jnp.stack([further, grouped[:, 1], nearer], axis=1)
    returned = (
        lax.all_to_all(
            regrouped.astype(jnp.bfloat16), "sub", split_axis=2, concat_axis=2, tiled=True
        )
        .astype(regrouped.dtype)
        .reshape(features, peer_count, halo_width)
    )
    masked = jnp.where(live_slots[None], returned, jnp.zeros_like(returned)).reshape(features, -1)
    local_delta = local_delta + column_scatter(masked, safe_index, cell_count)
    totals = lax.psum(
        (
            partials[0],
            partials[1],
            partials[2],
            partials[3],
            partials[4],
            partials[5],
            partials[6],
            partials[7],
            partials[8],
            partials[9],
        ),
        ("dom", "sub"),
    )
    faces_total = edge_state.shape[1] * lax.axis_size("dom") * sub_count
    factor = 1.0 / math.sqrt(faces_total)
    (
        edgefirst_sum,
        edgebias_sum,
        edgesecond_sum,
        edgegain_sum,
        edgeshift_sum,
        nodefirst_sum,
        nodebias_sum,
        nodesecond_sum,
        nodegain_sum,
        nodeshift_sum,
    ) = totals
    return (
        local_delta.astype(jnp.bfloat16),
        edge_result,
        edgefirst_sum * factor,
        edgebias_sum * factor,
        edgesecond_sum * factor,
        edgegain_sum * factor,
        edgeshift_sum * factor,
        nodefirst_sum * factor,
        nodebias_sum * factor,
        nodesecond_sum * factor,
        nodegain_sum * factor,
        nodeshift_sum * factor,
    )


def solution(mesh):
    in_specs = (
        P(None, ("dom", "sub")),
        P(None, ("dom", "sub")),
        P(("dom", "sub")),
        P(("dom", "sub")),
        P(("dom", "sub"), None, None),
        P(None, ("dom", "sub")),
        P(None, ("dom", "sub")),
        P(),
        P(),
        P(),
        P(),
        P(),
        P(),
        P(),
        P(),
        P(),
    )
    out_specs = (
        P(None, ("dom", "sub")),
        P(None, ("dom", "sub")),
        P(),
        P(),
        P(),
        P(),
        P(),
        P(),
        P(),
        P(),
        P(),
        P(),
    )
    return jax.shard_map(
        on_device, mesh=mesh, in_specs=in_specs, out_specs=out_specs, check_vma=False
    )
```

profile of v0, /device:TPU:0, one launch (start us, length us, event | category | flops | bytes accessed | tf_op | source)
XLA Modules:
  0.0 289.3 jit_solution(8450819076300327334)
XLA Ops:
  8.7 4.2 %while.108 = (s32[]{:T(128)}, bf16[64,1536]{1,0:T(8,128)(2,1)S(1)}, s32[3,512]{1,0:T(4,128)S(1)}, bf16[64,1024]{1,0:T(8,128)(2,1)}, s32[]{:T(128)}, /*index=5*/s32[]{:T(128)}, s32[]{:T(128)}, s32[]{:T(128)}) while((s32[]{:T(128)}, bf16[64,1536]{1,0:T(8,128)(2,1)S(1)}, s32[3,512]{1,0:T(4,128)S(1)}, bf16[64,1024]{1,0:T(8,128)(2,1)}, s32[]{:T(128)}, ...), condition=%wide.region_1.2_spmd, body=%wide.region_0.1_spmd.sunk | while | flops 67665928 | bytes 202891 | solution.py:89
  13.8 4.2 %all-to-all-start = ((bf16[64,3,4,128]{3,0,1,2:T(8,128)(2,1)}), bf16[64,3,4,128]{3,0,1,2:T(8,128)(2,1)S(1)}, u32[]{:S(2)}, u32[]{:S(2)}) async-start(bf16[64,3,4,128]{3,0,1,2:T(8,128)(2,1)} %copy.47), calls=%async_computation | async-start | bytes 393216 | tf_op jit(solution)/shard_map/all_to_all | solution.py:228
  18.1 5.3 %all-to-all-done = bf16[64,3,4,128]{3,0,1,2:T(8,128)(2,1)S(1)} async-done(((bf16[64,3,4,128]{3,0,1,2:T(8,128)(2,1)}), bf16[64,3,4,128]{3,0,1,2:T(8,128)(2,1)S(1)}, u32[]{:S(2)}, u32[]{:S(2)}) %all-to-all-start) | async-done | bytes 196640 | tf_op jit(solution)/shard_map/all_to_all | solution.py:228
  23.4 4.0 %collective-permute-start.1 = (bf16[64,4,128]{2,0,1:T(8,128)(2,1)S(1)}, bf16[64,4,128]{2,0,1:T(8,128)(2,1)S(1)}, u32[]{:S(2)}, u32[]{:S(2)}) collective-permute-start(bf16[64,4,128]{2,0,1:T(8,128)(2,1)S(1)} %get-tuple-element.818), channel_id=1, source_target_pairs={{0,4},{4,8},{8,12},{12,16},{16,20},{20,24},{24,28},{1,5},{5,9},{9,... | collective-permute-start | bytes 196616 | tf_op jit(solution)/shard_map/ppermute | solution.py:14
  28.8 3.0 %while.110 = (s32[]{:T(128)}, bf16[64,3072]{1,0:T(8,128)(2,1)S(1)}, s32[6,512]{1,0:T(8,128)S(1)}, bf16[64,1024]{1,0:T(8,128)(2,1)S(1)}, s32[]{:T(128)}, /*index=5*/s32[]{:T(128)}, s32[]{:T(128)}, s32[]{:T(128)}) while((s32[]{:T(128)}, bf16[64,3072]{1,0:T(8,128)(2,1)S(1)}, s32[6,512]{1,0:T(8,128)S(1)}, bf16[64,1024]{1,0:T(8,128)(2,1)S(1)}, ...), condition=%wide.region_5.6_spmd, body=%wide.region_4.5_spmd.sunk | while | flops 67665928 | bytes 202891 | solution.py:89
  31.9 1.7 collective-permute-done
  33.9 11.0 %while.109 = (s32[]{:T(128)}, bf16[64,3072]{1,0:T(8,128)(2,1)S(1)}, s32[6,512]{1,0:T(8,128)S(1)}, bf16[64,1024]{1,0:T(8,128)(2,1)S(1)}, bf16[64,1536]{1,0:T(8,12...) while((s32[]{:T(128)}, bf16[64,3072]{1,0:T(8,128)(2,1)S(1)}, s32[6,512]{1,0:T(8,128)S(1)}, ...), condition=%wide.region_3.4_spmd, body=%wide.region_2.3_spmd.sunk | while | flops 169248768 | bytes 1472659 | solution.py:89
  48.3 3.7 %while.112 = (s32[]{:T(128)}, f32[64,1024]{1,0:T(8,128)S(1)}, bf16[64,3072]{1,0:T(8,128)(2,1)S(1)}, s32[6,512]{1,0:T(8,128)S(1)}, s32[]{:T(128)}, /*index=5*/s32[]{:T(128)}, s32[]{:T(128)}, s32[]{:T(128)}) while((s32[]{:T(128)}, f32[64,1024]{1,0:T(8,128)S(1)}, bf16[64,3072]{1,0:T(8,128)(2,1)S(1)}, s32[6,512]{1,0:T(8,128)S(1)}, ...), condition=%wide.region_9.10_spmd.clone, body=%wide.region_8.9_spmd.clone.sunk | while | flops 67764232 | bytes 596117 | solution.py:110
  57.2 11.1 %while.111 = (s32[]{:T(128)}, f32[64,3072]{1,0:T(8,128)S(1)}, s32[6,512]{1,0:T(8,128)S(1)}, f32[64,1024]{1,0:T(8,128)}, s32[]{:T(128)}, /*index=5*/s32[]{:T(128)}, s32[]{:T(128)}, s32[]{:T(128)}) while((s32[]{:T(128)}, f32[64,3072]{1,0:T(8,128)S(1)}, s32[6,512]{1,0:T(8,128)S(1)}, f32[64,1024]{1,0:T(8,128)}, s32[]{:T(128)}, ...), condition=%wide.region_15.16_spmd, body=%wide.region_14.15_spmd.sunk | while | flops 403177472 | bytes 399499 | solution.py:89
  57.2 1.8 fusion.184
  59.1 1.8 fusion.184
  60.9 1.8 fusion.184
  62.8 1.8 fusion.184
  64.6 1.8 fusion.184
  66.5 1.8 fusion.184
  75.0 45.6 %while.113 = (s32[]{:T(128)}, f32[64,2560]{1,0:T(8,128)S(1)}, f32[64,3072]{1,0:T(8,128)}, s32[6,512]{1,0:T(8,128)S(1)}, s32[]{:T(128)}, /*index=5*/s32[]{:T(128)}, s32[]{:T(128)}, s32[]{:T(128)}) while((s32[]{:T(128)}, f32[64,2560]{1,0:T(8,128)S(1)}, f32[64,3072]{1,0:T(8,128)}, s32[6,512]{1,0:T(8,128)S(1)}, s32[]{:T(128)}, ...), condition=%wide.region_19.20_spmd.clone, body=%wide.region_18.19_spmd.clone.sunk | while | flops 1008273408 | bytes 3307685 | solution.py:110
  75.0 1.5 convolution_dynamic-update-slice_fusion.10
  97.8 1.5 convolution_dynamic-update-slice_fusion.10
  120.8 4.3 %collective-permute-start.2 = (bf16[64,4,128]{2,1,0:T(4,128)(2,1)S(1)}, bf16[64,4,128]{2,1,0:T(4,128)(2,1)S(1)}, u32[]{:S(2)}, u32[]{:S(2)}) collective-permute-start(bf16[64,4,128]{2,1,0:T(4,128)(2,1)S(1)} %get-tuple-element.814), channel_id=1, source_target_pairs={{0,4},{4,8},{8,12},{12,16},{16,20},{20,24},{24,28},{1,5},{5,9},{9,... | collective-permute-start | bytes 196616 | tf_op jit(solution)/shard_map/ppermute | solution.py:14
  126.6 6.2 %while.114 = (s32[]{:T(128)}, f32[64,1024]{1,0:T(8,128)S(1)}, f32[64,3072]{1,0:T(8,128)S(1)}, s32[6,512]{1,0:T(8,128)S(1)}, s32[]{:T(128)}, /*index=5*/s32[]{:T(128)}, s32[]{:T(128)}, s32[]{:T(128)}) while((s32[]{:T(128)}, f32[64,1024]{1,0:T(8,128)S(1)}, f32[64,3072]{1,0:T(8,128)S(1)}, s32[6,512]{1,0:T(8,128)S(1)}, s32[]{:T(128)}, ...), condition=%wide.region_21.22_spmd.clone, body=%wide.region_20.21_spmd.clone.sunk | while | flops 403308544 | bytes 661653 | solution.py:110
  132.9 124.5 %all-reduce.3.cloned.1.call-done = (f32[192,64]{0,1:T(8,128)}, f32[64]{0:T(128)}, f32[64,64]{1,0:T(8,128)}, f32[64]{0:T(128)}, f32[64]{0:T(128)}, /*index=5*/f32...) async-done(((f32[192,64]{0,1:T(8,128)}, f32[64]{0:T(128)}, f32[64,64]{1,0:T(8,128)}, f32[64]{0:T(128)}, f32[64]{0:T(128)}, ...) | async-done | bytes 116240 | tf_op jit(solution)/shard_map/psum | solution.py:267
  269.6 3.4 %all-to-all-start.1 = ((bf16[64,3,4,128]{3,0,1,2:T(8,128)(2,1)}), bf16[64,3,4,128]{3,0,1,2:T(8,128)(2,1)S(1)}, u32[]{:S(2)}, u32[]{:S(2)}) async-start(bf16[64,3,4,128]{3,0,1,2:T(8,128)(2,1)} %copy.54), calls=%async_computation.1 | async-start | bytes 393216 | tf_op jit(solution)/shard_map/all_to_all | solution.py:259
  274.1 4.1 %all-to-all-done.1 = bf16[64,3,4,128]{3,0,1,2:T(8,128)(2,1)S(1)} async-done(((bf16[64,3,4,128]{3,0,1,2:T(8,128)(2,1)}), bf16[64,3,4,128]{3,0,1,2:T(8,128)(2,1)S(1)}, u32[]{:S(2)}, u32[]{:S(2)}) %all-to-all-start.1) | async-done | bytes 196640 | tf_op jit(solution)/shard_map/all_to_all | solution.py:259
  278.6 3.1 %while.115 = (s32[]{:T(128)}, f32[64,1024]{1,0:T(8,128)S(1)}, f32[64,1536]{1,0:T(8,128)S(1)}, s32[3,512]{1,0:T(4,128)S(1)}, s32[]{:T(128)}, /*index=5*/s32[]{:T(128)}, s32[]{:T(128)}, s32[]{:T(128)}) while((s32[]{:T(128)}, f32[64,1024]{1,0:T(8,128)S(1)}, f32[64,1536]{1,0:T(8,128)S(1)}, s32[3,512]{1,0:T(4,128)S(1)}, s32[]{:T(128)}, ...), condition=%wide.region_23.24_spmd.clone, body=%wide.region_22.23_spmd.clone.sunk | while | flops 403308544 | bytes 661653 | solution.py:110
  (302 shorter events, 107.2 us)
Async XLA Ops:
  7.2 37.9 %copy-start = (bf16[192,64]{0,1:T(8,128)(2,1)S(1)}, bf16[192,64]{0,1:T(8,128)(2,1)}, u32[]{:S(2)}) copy-start(bf16[192,64]{0,1:T(8,128)(2,1)} %param.39) | copy-start | bytes 73732
  8.7 9.4 %copy-start.13 = (s32[3072]{0:T(1024)S(1)}, s32[3072]{0:T(1024)}, u32[]{:S(2)}) copy-start(s32[3072]{0:T(1024)} %param.35) | copy-start | bytes 36868
  12.9 15.8 %copy-start.18 = (bf16[64,1024]{1,0:T(8,128)(2,1)S(1)}, bf16[64,1024]{1,0:T(8,128)(2,1)}, u32[]{:S(2)}) copy-start(bf16[64,1024]{1,0:T(8,128)(2,1)} %get-tuple-element.1290) | copy-start | bytes 393220
  13.8 9.5 %all-to-all-start = ((bf16[64,3,4,128]{3,0,1,2:T(8,128)(2,1)}), bf16[64,3,4,128]{3,0,1,2:T(8,128)(2,1)S(1)}, u32[]{:S(2)}, u32[]{:S(2)}) async-start(bf16[64,3,4,128]{3,0,1,2:T(8,128)(2,1)} %copy.47), calls=%async_computation | async-start | bytes 393216 | tf_op jit(solution)/shard_map/all_to_all | solution.py:228
  18.1 239.3 %all-reduce.3.cloned.1.call-start = ((), (), s32[]{:S(2)}) async-start(), calls=%async_computation.2 | async-start | bytes 333824 | tf_op jit(solution)/shard_map/psum | solution.py:267
  23.4 8.5 %collective-permute-start.1 = (bf16[64,4,128]{2,0,1:T(8,128)(2,1)S(1)}, bf16[64,4,128]{2,0,1:T(8,128)(2,1)S(1)}, u32[]{:S(2)}, u32[]{:S(2)}) collective-permute-start(bf16[64,4,128]{2,0,1:T(8,128)(2,1)S(1)} %get-tuple-element.818), channel_id=1, source_target_pairs={{0,4},{4,8},{8,12},{12,16},{16,20},{20,24},{24,28},{1,5},{5,9},{9,... | collective-permute-start | bytes 196616 | tf_op jit(solution)/shard_map/ppermute | solution.py:14
  27.4 6.2 %collective-permute-start = (bf16[64,4,128]{2,0,1:T(8,128)(2,1)S(1)}, bf16[64,4,128]{2,0,1:T(8,128)(2,1)S(1)}, u32[]{:S(2)}, u32[]{:S(2)}) collective-permute-start(bf16[64,4,128]{2,0,1:T(8,128)(2,1)S(1)} %get-tuple-element.817), channel_id=1, source_target_pairs={{4,0},{8,4},{12,8},{16,12},{20,16},{24,20},{28,24},{5,1},{9,5},{13... | collective-permute-start | bytes 196616 | tf_op jit(solution)/shard_map/ppermute | solution.py:14
  28.8 3.1 %copy-start.14 = (s32[3072]{0:T(1024)S(1)}, s32[3072]{0:T(1024)}, u32[]{:S(2)}) copy-start(s32[3072]{0:T(1024)} %param.34) | copy-start | bytes 36868
  33.9 11.1 %copy-start.7 = (bf16[64,3072]{1,0:T(8,128)(2,1)S(1)}, bf16[64,3072]{1,0:T(8,128)(2,1)}, u32[]{:S(2)}) copy-start(bf16[64,3072]{1,0:T(8,128)(2,1)} %param.33) | copy-start | bytes 1179652
  45.6 1.3 copy-start.2
  45.6 2.0 copy-start.10
  45.6 2.5 copy-start.15
  45.6 2.5 copy-start.17
  48.3 3.8 %copy-start.12 = (bf16[128,64]{0,1:T(8,128)(2,1)S(1)}, bf16[128,64]{0,1:T(8,128)(2,1)}, u32[]{:S(2)}) copy-start(bf16[128,64]{0,1:T(8,128)(2,1)} %param.44) | copy-start | bytes 49156
  48.3 3.8 %copy-start.20 = (f32[64]{0:T(128)S(1)}, f32[64]{0:T(128)}, u32[]{:S(2)}) copy-start(f32[64]{0:T(128)} %param.45) | copy-start | bytes 772
  48.3 4.0 %copy-start.11 = (bf16[64,64]{1,0:T(8,128)(2,1)S(1)}, bf16[64,64]{1,0:T(8,128)(2,1)}, u32[]{:S(2)}) copy-start(bf16[64,64]{1,0:T(8,128)(2,1)} %param.46) | copy-start | bytes 24580
  57.2 11.2 %copy-start.1 = (bf16[64,3072]{1,0:T(8,128)(2,1)S(1)}, bf16[64,3072]{1,0:T(8,128)(2,1)}, u32[]{:S(2)}) copy-start(bf16[64,3072]{1,0:T(8,128)(2,1)} %param.38) | copy-start | bytes 1179652
  68.3 1.7 copy-start.5
  70.9 1.3 copy-start.3
  75.0 51.6 %copy-start.9 = (f32[64,1024]{1,0:T(8,128)S(1)}, f32[64,1024]{1,0:T(8,128)}, u32[]{:S(2)}) copy-start(f32[64,1024]{1,0:T(8,128)} %custom-call.2) | copy-start | bytes 786436
  120.8 147.9 %collective-permute-start.2 = (bf16[64,4,128]{2,1,0:T(4,128)(2,1)S(1)}, bf16[64,4,128]{2,1,0:T(4,128)(2,1)S(1)}, u32[]{:S(2)}, u32[]{:S(2)}) collective-permute-start(bf16[64,4,128]{2,1,0:T(4,128)(2,1)S(1)} %get-tuple-element.814), channel_id=1, source_target_pairs={{0,4},{4,8},{8,12},{12,16},{16,20},{20,24},{24,28},{1,5},{5,9},{9,... | collective-permute-start | bytes 196616 | tf_op jit(solution)/shard_map/ppermute | solution.py:14
  125.1 143.6 %collective-permute-start.3 = (bf16[64,4,128]{2,1,0:T(4,128)(2,1)S(1)}, bf16[64,4,128]{2,1,0:T(4,128)(2,1)S(1)}, u32[]{:S(2)}, u32[]{:S(2)}) collective-permute-start(bf16[64,4,128]{2,1,0:T(4,128)(2,1)S(1)} %get-tuple-element.815), channel_id=1, source_target_pairs={{4,0},{8,4},{12,8},{16,12},{20,16},{24,20},{28,24},{5,1},{9,5},{13... | collective-permute-start | bytes 196616 | tf_op jit(solution)/shard_map/ppermute | solution.py:14
  132.8 145.7 %copy-start.8 = (f32[64,1024]{1,0:T(8,128)S(1)}, f32[64,1024]{1,0:T(8,128)}, u32[]{:S(2)}) copy-start(f32[64,1024]{1,0:T(8,128)} %custom-call.3) | copy-start | bytes 786436
  269.6 8.6 %all-to-all-start.1 = ((bf16[64,3,4,128]{3,0,1,2:T(8,128)(2,1)}), bf16[64,3,4,128]{3,0,1,2:T(8,128)(2,1)S(1)}, u32[]{:S(2)}, u32[]{:S(2)}) async-start(bf16[64,3,4,128]{3,0,1,2:T(8,128)(2,1)} %copy.54), calls=%async_computation.1 | async-start | bytes 393216 | tf_op jit(solution)/shard_map/all_to_all | solution.py:259
  (5 other events, 4.4 us)
Sparse Core Ops, SparseCore 0:
  126.7 130.6 all-reduce.2
where the time goes:
time: 291 us; the launch traced here: 289 us
  waiting for transfers between devices  136 us (47%)
  matrix products  92.7 us (32%)
  other arithmetic  20.3 us (7%)
  starting transfers between devices  18.7 us (6%)
  between operations  14.6 us (5%)
  local copies, waits for them, and re-layouts  5.33 us (2%)
    psum x1, waiting for transfers between devices, on_device(): lax.psum((partials[0], partials[1], partials[2], partials[3], partials[4]...  125 us
    dot_general x45, matrix products, one_block(): jnp.dot(portion, selector, precision=precision, preferred_element_type=jn...  56.2 us
    dot_general x45, matrix products, one_block(): jnp.dot(table[:, begin:begin + piece], selector, precision=precision, pre...  28.1 us
    ppermute x4, starting transfers between devices, from_behind(): lax.ppermute(value, axis, [(source, source + steps) for source in range(f...  11.1 us
  transfers between devices with their start and end apart: 7, of which 4 were waited for; matrix products, arithmetic and copies ran while one was open for 7% of the time, Pallas kernels for 0%

commit v1 on v0

v1 whole, which is shorter than its diff:
```python
import functools
import math

import jax
import jax.numpy as jnp
from jax import lax
from jax.experimental import pallas as pl
from jax.experimental.pallas import tpu as pltpu
from jax.sharding import PartitionSpec as P

EPSILON = 1e-05
MESH = pl.DeviceIdType.MESH
BF = jnp.bfloat16
F32 = jnp.float32


def nn(a, b):
    return lax.dot_general(a, b, (((1,), (0,)), ((), ())), preferred_element_type=F32)


def nt(a, b):
    return lax.dot_general(a, b, (((1,), (1,)), ((), ())), preferred_element_type=F32)


def flip(a):
    return a.astype(F32).T


def one_hot(index, rows):
    return jnp.where(lax.broadcasted_iota(jnp.int32, (rows, index.shape[1]), 0) == index, 1.0, 0.0).astype(BF)


def standardize(values):
    centered = values - jnp.mean(values, axis=0, keepdims=True)
    spread = lax.rsqrt(jnp.mean(centered * centered, axis=0, keepdims=True) + EPSILON)
    return centered * spread, spread


def normalize_back(upstream, scaled, spread, gain):
    weighted = upstream * gain
    return spread * (
        weighted
        - jnp.mean(weighted, axis=0, keepdims=True)
        - scaled * jnp.mean(weighted * scaled, axis=0, keepdims=True)
    )


def packed_rows(features):
    half = 3 * features // 2
    return half, half + features, half + 2 * features


def fold_lanes(values):
    total = values[:, :128]
    for begin in range(128, values.shape[1], 128):
        total = total + values[:, begin : begin + 128]
    return total


def halo_peers(dom, sub):
    d, s = lax.axis_index("dom"), lax.axis_index("sub")
    for o in (0, 2, 1):
        for r in range(sub):
            if o == 1 and r == 0:
                continue
            t = lax.rem(s + r, sub)
            target = d + (o - 1)
            yield o, t, target, (target >= 0) & (target < dom)


def halo_barrier_signal(dom, sub, barrier):
    for o, t, target, there in halo_peers(dom, sub):
        if o == 1:
            pl.semaphore_signal(barrier, inc=1, device_id=(target, t), device_id_type=MESH)
        else:
            @pl.when(there)
            def _():
                pl.semaphore_signal(barrier, inc=1, device_id=(target, t), device_id_type=MESH)


def halo_barrier_count(dom, sub):
    d = lax.axis_index("dom")
    ends = jnp.where(d > 0, sub, 0) + jnp.where(d < dom - 1, sub, 0)
    return ends + (sub - 1)


def pick_kernel(dom, sub, node_ref, index_ref, ghost_ref, outgoing, incoming, send_sem, recv_sem):
    d, s = lax.axis_index("dom"), lax.axis_index("sub")
    barrier = pltpu.get_barrier_semaphore()
    halo_barrier_signal(dom, sub, barrier)
    cells = node_ref.shape[1]
    halo = outgoing.shape[2]

    def pick(number, carry):
        chosen = index_ref[:, pl.ds(pl.multiple_of(number * 2 * halo, 2 * halo), 2 * halo)]
        picked = nn(node_ref[...], one_hot(chosen, cells)).astype(BF)
        outgoing[2 * number] = picked[:, :halo]
        outgoing[2 * number + 1] = picked[:, halo:]
        return carry

    lax.fori_loop(0, outgoing.shape[0] // 2, pick, 0)
    pl.semaphore_wait(barrier, halo_barrier_count(dom, sub))
    exchange(dom, sub, d, s, outgoing, incoming, send_sem, recv_sem, forward=True)
    for k in range(3 * sub):
        ghost_ref[:, k * halo : (k + 1) * halo] = incoming[k]


def halo_copy(outgoing, incoming, send_sem, recv_sem, source, landing, target, t):
    return pltpu.make_async_remote_copy(
        src_ref=outgoing.at[source],
        dst_ref=incoming.at[landing],
        send_sem=send_sem.at[source],
        recv_sem=recv_sem.at[landing],
        device_id=(target, t),
        device_id_type=MESH,
    )


def guarded(o, there, action):
    if o == 1:
        action()
    else:
        pl.when(there)(action)


def start_exchange(dom, sub, s, outgoing, incoming, send_sem, recv_sem, forward):
    for o, t, target, there in halo_peers(dom, sub):
        block = o if forward else 2 - o

        def start(block=block, t=t, target=target):
            halo_copy(outgoing, incoming, send_sem, recv_sem, block * sub + t, block * sub + s, target, t).start()

        guarded(o, there, start)
    d = lax.axis_index("dom")
    incoming[sub + s] = jnp.zeros(incoming.shape[1:], incoming.dtype)
    for o in (0, 2):
        origin = d + 1 - o if forward else d + o - 1

        @pl.when((origin < 0) | (origin >= dom))
        def _():
            for u in range(sub):
                incoming[o * sub + u] = jnp.zeros(incoming.shape[1:], incoming.dtype)


def finish_exchange(dom, sub, s, outgoing, incoming, send_sem, recv_sem, forward):
    for o, t, target, there in halo_peers(dom, sub):
        block = 2 - o if forward else o

        def finish(block=block, t=t, target=target):
            halo_copy(outgoing, incoming, send_sem, recv_sem, block * sub + t, block * sub + t, target, t).wait_recv()

        guarded(o, there, finish)
    for o, t, target, there in halo_peers(dom, sub):
        block = o if forward else 2 - o

        def finish(block=block, t=t, target=target):
            halo_copy(outgoing, incoming, send_sem, recv_sem, block * sub + t, block * sub + t, target, t).wait_send()

        guarded(o, there, finish)


def exchange(dom, sub, d, s, outgoing, incoming, send_sem, recv_sem, forward):
    start_exchange(dom, sub, s, outgoing, incoming, send_sem, recv_sem, forward)
    finish_exchange(dom, sub, s, outgoing, incoming, send_sem, recv_sem, forward)


def local_kernel(
    chunk,
    node_ref, ghost_ref, edge_ref, senders_ref, receivers_ref, node_cot_ref, edge_cot_ref,
    edge_first_ref, edge_second_ref, node_first_ref, node_second_ref, columns_ref,
    local_ref, ghost_delta_ref, edge_out_ref, packed_ref,
    selector, extended, slope, active, scaled_all, spread_all, summed, sums, small, lanes,
):
    features, cells = node_ref.shape
    faces = edge_ref.shape[1]
    ghosts = ghost_ref.shape[1]
    width = cells + ghosts
    step = 64
    extended[:, :cells] = node_ref[...]
    extended[:, cells:] = ghost_ref[...]
    edge_first_t = flip(edge_first_ref[...]).astype(BF)
    edge_second_t = flip(edge_second_ref[...]).astype(BF)
    edge_bias = columns_ref[:, 0:1]
    edge_gain = columns_ref[:, 1:2]
    edge_shift = columns_ref[:, 2:3]
    node_bias = columns_ref[:, 3:4]
    node_gain = columns_ref[:, 4:5]
    summed[...] = jnp.zeros(summed.shape, F32)
    row = lax.broadcasted_iota(jnp.int32, (step, chunk), 0)

    def forward(c, carry):
        here = pl.ds(pl.multiple_of(c * chunk, chunk), chunk)
        sender = senders_ref[:, here]
        receiver = receivers_ref[:, here]

        def fill(begin, index):
            def body(i, inner):
                at = pl.multiple_of(i * step, step)
                hit = row == (index - at)
                selector[c, pl.ds(pl.multiple_of(begin + at, step), step), :] = jnp.where(hit, 1.0, 0.0).astype(BF)
                return inner
            return body

        lax.fori_loop(0, width // step, fill(0, sender), 0)
        lax.fori_loop(0, cells // step, fill(width, receiver), 0)
        sent = nn(extended[...], selector[c, :width, :]).astype(BF)
        received = nn(node_ref[...], selector[c, width:, :]).astype(BF)
        stacked = jnp.concatenate([sent, received, edge_ref[:, here]], axis=0)
        linear = nn(edge_first_t, stacked) + edge_bias
        logistic = jax.nn.sigmoid(linear)
        lively = (linear * logistic).astype(BF)
        slope[:, here] = logistic * (1.0 + linear * (1.0 - logistic))
        active[:, here] = lively
        scaled, spread = standardize(nn(edge_second_t, lively))
        scaled_all[:, here] = scaled
        spread_all[:, here] = spread
        message = (scaled * edge_gain + edge_shift).astype(BF)
        summed[...] += nt(selector[c, width:, :], message)
        return carry

    lax.fori_loop(0, faces // chunk, forward, 0)

    node_first_t = flip(node_first_ref[...]).astype(BF)
    node_second_t = flip(node_second_ref[...]).astype(BF)
    node_input = jnp.concatenate([node_ref[...], summed[...].T.astype(BF)], axis=0)
    node_linear = nn(node_first_t, node_input) + node_bias
    node_logistic = jax.nn.sigmoid(node_linear)
    node_active = (node_linear * node_logistic).astype(BF)
    node_scaled, node_spread = standardize(nn(node_second_t, node_active))
    upstream = node_cot_ref[...].astype(F32)
    lanes[3] = fold_lanes(upstream * node_scaled)
    lanes[4] = fold_lanes(upstream)
    node_delta = normalize_back(upstream, node_scaled, node_spread, node_gain).astype(BF)
    node_slope = node_logistic * (1.0 + node_linear * (1.0 - node_logistic))
    node_hidden = nn(node_second_ref[...], node_delta) * node_slope
    lanes[5] = fold_lanes(node_hidden)
    node_hidden = node_hidden.astype(BF)
    node_first_delta = nt(node_input, node_hidden)
    half, mid, top = packed_rows(features)
    packed_ref[half:mid, :features] = node_first_delta[:features]
    packed_ref[half:mid, features:] = node_first_delta[features:]
    packed_ref[mid:top, features:] = nt(node_active, node_delta)
    node_back = nn(node_first_ref[...], node_hidden)
    local_ref[...] = node_back[:features] + upstream
    toward = node_back[features:]
    high = toward.astype(BF)
    low = (toward - high.astype(F32)).astype(BF)
    toward = jnp.concatenate([high, low], axis=0)

    sums[...] = jnp.zeros(sums.shape, F32)
    small[...] = jnp.zeros(small.shape, F32)
    for i in range(3):
        lanes[i] = jnp.zeros(lanes.shape[1:], F32)

    def backward(c, carry):
        here = pl.ds(pl.multiple_of(c * chunk, chunk), chunk)
        gathered = nn(toward, selector[c, width:, :])
        cotangent = edge_cot_ref[:, here].astype(F32)
        delta = cotangent + (gathered[:features] + gathered[features:])
        scaled = scaled_all[:, here]
        lanes[0] += fold_lanes(delta * scaled)
        lanes[1] += fold_lanes(delta)
        edge_delta = normalize_back(delta, scaled, spread_all[:, here], edge_gain).astype(BF)
        small[0] += nt(active[:, here], edge_delta)
        hidden = nn(edge_second_ref[...], edge_delta) * slope[:, here]
        lanes[2] += fold_lanes(hidden)
        hidden = hidden.astype(BF)
        edge_out_ref[:, here] = (cotangent + nn(edge_first_ref[2 * features :, :], hidden)).astype(BF)
        small[1] += nt(edge_ref[:, here], hidden)
        sums[...] += nt(selector[c], hidden)
        return carry

    lax.fori_loop(0, faces // chunk, backward, 0)

    by_sender = sums[:width, :].astype(BF)
    by_receiver = sums[width:, :].astype(BF)
    first = nn(extended[...], by_sender)
    second = nn(node_ref[...], by_receiver)
    packed_ref[0:features, :features] = first
    packed_ref[features:half, :features] = second[: half - features]
    packed_ref[0 : 2 * features - half, features:] = second[half - features :]
    packed_ref[2 * features - half : half, features:] = small[1]
    packed_ref[mid:top, :features] = small[0]
    column = lax.broadcasted_iota(jnp.int32, (features, 128), 1)
    vectors = jnp.zeros((features, 128), F32)
    for i in range(6):
        vectors = jnp.where(column == i, jnp.sum(lanes[i], axis=1, keepdims=True), vectors)
    packed_ref[top:, :] = jnp.zeros((packed_ref.shape[0] - top, 128), F32)
    packed_ref[top : top + 8, :features] = vectors.T[:8]
    back = nt(edge_first_ref[:features, :], by_sender)
    local_ref[...] += back[:, :cells] + nt(edge_first_ref[features : 2 * features, :], by_receiver)
    halo = ghost_delta_ref.shape[2]
    for k in range(ghosts // halo):
        ghost_delta_ref[k] = back[:, cells + k * halo : cells + (k + 1) * halo].astype(BF)


def finish_kernel(
    dom, sub, factor,
    ghost_ref, local_ref, index_ref, packed_ref,
    state_ref, edge_first_ref, edge_second_ref, node_first_ref, node_second_ref, vectors_ref,
    incoming, selector, scattered, pieces, reduced, gathered,
    send_sem, recv_sem, part_send, part_recv, whole_send, whole_recv,
):
    d, s = lax.axis_index("dom"), lax.axis_index("sub")
    count = dom * sub
    me = d * sub + s
    rows = reduced.shape[0]
    barrier = pltpu.get_barrier_semaphore()

    def place(r):
        other = lax.rem(me + r, count)
        return other, (other // sub, lax.rem(other, sub))

    def greet(r, carry):
        _, device = place(r)
        pl.semaphore_signal(barrier, inc=1, device_id=device, device_id_type=MESH)
        return carry

    lax.fori_loop(1, count, greet, 0)
    pl.semaphore_wait(barrier, count - 1)
    start_exchange(dom, sub, s, ghost_ref, incoming, send_sem, recv_sem, forward=False)

    def part_copy(source, landing, device):
        return pltpu.make_async_remote_copy(
            src_ref=packed_ref.at[pl.ds(pl.multiple_of(source * rows, 8), rows)],
            dst_ref=pieces.at[landing],
            send_sem=part_send.at[source],
            recv_sem=part_recv.at[landing],
            device_id=device,
            device_id_type=MESH,
        )

    def whole_copy(landing, device, other):
        return pltpu.make_async_remote_copy(
            src_ref=reduced,
            dst_ref=gathered.at[pl.ds(pl.multiple_of(landing * rows, 8), rows)],
            send_sem=whole_send.at[other],
            recv_sem=whole_recv.at[landing],
            device_id=device,
            device_id_type=MESH,
        )

    def send_part(r, carry):
        other, device = place(r)
        part_copy(other, me, device).start()
        return carry

    lax.fori_loop(1, count, send_part, 0)
    cells = state_ref.shape[1]
    span = selector.shape[2]

    def build(i, carry):
        selector[i] = one_hot(index_ref[:, pl.ds(pl.multiple_of(i * span, span), span)], cells)
        return carry

    lax.fori_loop(0, selector.shape[0], build, 0)
    own = pl.ds(pl.multiple_of(me * rows, 8), rows)

    def take_part(r, total):
        other, device = place(r)
        part_copy(other, other, device).wait_recv()
        return total + pieces[other]

    reduced[...] = lax.fori_loop(1, count, take_part, packed_ref[own, :])

    def send_whole(r, carry):
        other, device = place(r)
        whole_copy(me, device, other).start()
        return carry

    lax.fori_loop(1, count, send_whole, 0)
    gathered[own, :] = reduced[...]
    finish_exchange(dom, sub, s, ghost_ref, incoming, send_sem, recv_sem, forward=False)
    scattered[...] = jnp.zeros(scattered.shape, F32)

    def scatter(i, carry):
        value = jnp.concatenate([incoming[2 * i], incoming[2 * i + 1]], axis=1)
        scattered[...] += nt(selector[i], value)
        return carry

    lax.fori_loop(0, selector.shape[0], scatter, 0)
    state_ref[...] = (local_ref[...] + scattered[...].T).astype(BF)

    def settle(r, carry):
        other, device = place(r)
        whole_copy(other, device, other).wait_recv()
        return carry

    lax.fori_loop(1, count, settle, 0)

    def settle_sends(r, carry):
        other, device = place(r)
        part_copy(other, other, device).wait_send()
        whole_copy(other, device, other).wait_send()
        return carry

    lax.fori_loop(1, count, settle_sends, 0)
    features = node_second_ref.shape[0]
    half, mid, top = packed_rows(features)
    edge_first_ref[:half, :] = gathered[0:half, :features] * factor
    edge_first_ref[half:, :] = gathered[0:half, features:] * factor
    node_first_ref[:features, :] = gathered[half:mid, :features] * factor
    node_first_ref[features:, :] = gathered[half:mid, features:] * factor
    edge_second_ref[...] = gathered[mid:top, :features] * factor
    node_second_ref[...] = gathered[mid:top, features:] * factor
    vectors_ref[...] = gathered[top : top + 8, :features] * factor


def on_device(
    dom, sub,
    node_state, edge_state, senders, receivers, send_index, node_cotangent, edge_cotangent,
    edge_first, edge_bias, edge_second, edge_gain, edge_shift, node_first, node_bias, node_second, node_gain,
):
    features, cells = node_state.shape
    faces = edge_state.shape[1]
    halo = send_index.shape[2]
    peers = 3 * sub
    ghosts = peers * halo
    width = cells + ghosts
    count = dom * sub
    rows = -(-(packed_rows(features)[2] + 8) // (8 * count)) * 8
    chunk = math.gcd(faces, 512)
    vmem = pl.BlockSpec(memory_space=pltpu.VMEM)
    shape = jax.ShapeDtypeStruct
    dma = pltpu.SemaphoreType.DMA
    index_row = send_index.reshape(1, ghosts)
    ghost = pl.pallas_call(
        functools.partial(pick_kernel, dom, sub),
        out_shape=shape((features, ghosts), BF),
        in_specs=[vmem] * 2,
        out_specs=vmem,
        scratch_shapes=[
            pltpu.VMEM((peers, features, halo), BF),
            pltpu.VMEM((peers, features, halo), BF),
            dma((peers,)),
            dma((peers,)),
        ],
        compiler_params=pltpu.CompilerParams(collective_id=0, has_side_effects=True),
        name="halo_out",
    )(node_state, index_row)
    columns = jnp.stack([edge_bias, edge_gain, edge_shift, node_bias, node_gain], axis=1)
    local, ghost_delta, edge_result, packed = pl.pallas_call(
        functools.partial(local_kernel, chunk),
        out_shape=(
            shape((features, cells), F32),
            shape((peers, features, halo), BF),
            shape((features, faces), BF),
            shape((count * rows, 128), F32),
        ),
        in_specs=[vmem] * 12,
        out_specs=(vmem,) * 4,
        scratch_shapes=[
            pltpu.VMEM((faces // chunk, width + cells, chunk), BF),
            pltpu.VMEM((features, width), BF),
            pltpu.VMEM((features, faces), F32),
            pltpu.VMEM((features, faces), BF),
            pltpu.VMEM((features, faces), F32),
            pltpu.VMEM((1, faces), F32),
            pltpu.VMEM((cells, features), F32),
            pltpu.VMEM((width + cells, features), F32),
            pltpu.VMEM((2, features, features), F32),
            pltpu.VMEM((6, features, 128), F32),
        ],
        compiler_params=pltpu.CompilerParams(vmem_limit_bytes=60 * 1024 * 1024),
        name="local_layer",
    )(
        node_state, ghost, edge_state, senders.reshape(1, faces), receivers.reshape(1, faces),
        node_cotangent, edge_cotangent, edge_first, edge_second, node_first, node_second, columns,
    )
    state, edge_first_sum, edge_second_sum, node_first_sum, node_second_sum, vectors = pl.pallas_call(
        functools.partial(finish_kernel, dom, sub, 1.0 / math.sqrt(faces * count)),
        out_shape=(
            shape((features, cells), BF),
            shape(edge_first.shape, F32),
            shape(edge_second.shape, F32),
            shape(node_first.shape, F32),
            shape(node_second.shape, F32),
            shape((8, features), F32),
        ),
        in_specs=[vmem] * 4,
        out_specs=(vmem,) * 6,
        scratch_shapes=[
            pltpu.VMEM((peers, features, halo), BF),
            pltpu.VMEM((peers // 2, cells, 2 * halo), BF),
            pltpu.VMEM((cells, features), F32),
            pltpu.VMEM((count, rows, 128), F32),
            pltpu.VMEM((rows, 128), F32),
            pltpu.VMEM((count * rows, 128), F32),
            dma((peers,)),
            dma((peers,)),
            dma((count,)),
            dma((count,)),
            dma((count,)),
            dma((count,)),
        ],
        compiler_params=pltpu.CompilerParams(collective_id=1, has_side_effects=True),
        name="halo_back_and_sum",
    )(ghost_delta, local, index_row, packed)
    return (
        state, edge_result, edge_first_sum, vectors[2], edge_second_sum, vectors[0], vectors[1],
        node_first_sum, vectors[5], node_second_sum, vectors[3], vectors[4],
    )


def solution(mesh):
    split = P(None, ("dom", "sub"))
    faces = P(("dom", "sub"))
    return jax.shard_map(
        functools.partial(on_device, mesh.shape["dom"], mesh.shape["sub"]),
        mesh=mesh,
        in_specs=(split, split, faces, faces, P(("dom", "sub"), None, None), split, split) + (P(),) * 9,
        out_specs=(split, split) + (P(),) * 10,
        check_vma=False,
    )
```

time: 291 us -> 68.1 us (0.23)
  waiting for transfers between devices: 136 us -> 0 us
  matrix products: 92.7 us -> 0 us
  Pallas kernels: 0 us -> 58.1 us
  other arithmetic: 20.3 us -> 0 us
  starting transfers between devices: 18.7 us -> 0 us
  between operations: 14.6 us -> 0.72 us
  local copies, waits for them, and re-layouts: 5.33 us -> 8.76 us
    psum x1 -> x0, waiting for transfers between devices: 125 us -> none  [on_device(): lax.psum((partials[0], partials[1], partials[2], partials[3], partials[4]...]
    dot_general x102 -> x0, matrix products: 92.7 us -> none  [the longest x45 56.2 us: one_block(): jnp.dot(portion, selector, precision=precision, preferred_element_type=jn...]
    pallas_call x0 -> x3, Pallas kernels: none -> 58.1 us  [the longest x1 28.5 us: on_device(): pl.pallas_call(functools.partial(local_kernel, chunk), out_shape=(shape((...]
    mul x10 -> x0, other arithmetic: 12.4 us -> none  [the longest x1 1.47 us: on_device(): edgefirst_sum * factor]
    ppermute x4 -> x0, starting transfers between devices: 11.1 us -> none  [from_behind(): lax.ppermute(value, axis, [(source, source + steps) for source in range(f...]
    all_to_all x2 -> x0, waiting for transfers between devices: 9.44 us -> none  [the longest x1 5.29 us: on_device(): lax.all_to_all(blocks, 'sub', split_axis=2, concat_axis=2, tiled=True)]
    all_to_all x2 -> x0, starting transfers between devices: 7.6 us -> none  [the longest x1 4.23 us: on_device(): lax.all_to_all(blocks, 'sub', split_axis=2, concat_axis=2, tiled=True)]
    unnamed x46 -> x29, local copies, waits for them, and re-layouts: 1.91 us -> 6.59 us
  transfers between devices with their start and end apart: 7 -> 0, of which waited for: 4 -> 0; matrix products, arithmetic and copies ran while one was open for 7% -> 0% of each run, Pallas kernels for 0% -> 0%
where the time goes in v1:
time: 68.1 us; the launch traced here: 67.6 us
  Pallas kernels  58.1 us (85%)
  local copies, waits for them, and re-layouts  8.76 us (13%)
  between operations  0.72 us (1%)
    pallas_call x1, Pallas kernels, on_device(): pl.pallas_call(functools.partial(local_kernel, chunk), out_shape=(shape((...  28.5 us
    pallas_call x1, Pallas kernels, on_device(): pl.pallas_call(functools.partial(finish_kernel, dom, sub, 1.0 / math.sqrt...  20.1 us
    pallas_call x1, Pallas kernels, on_device(): pl.pallas_call(functools.partial(pick_kernel, dom, sub), out_shape=shape(...  9.47 us
    unnamed x29, local copies, waits for them, and re-layouts  6.59 us
    squeeze x1, local copies, waits for them, and re-layouts, on_device(): vectors[4]  1.43 us

profile of v1, /device:TPU:0, one launch (start us, length us, event | category | flops | bytes accessed | tf_op | source)
XLA Modules:
  0.0 67.6 jit_solution(18116420399100663126)
XLA Ops:
  0.6 0.0 copy-start.9
  0.7 0.0 copy-start.10
  0.7 0.0 copy-start.6
  0.7 0.0 copy-start.7
  0.7 0.6 copy-done.9
  1.3 0.0 copy-done.10
  1.3 0.0 copy-done.6
  1.3 0.0 copy-done.7
  1.3 0.0 copy-done.8
  1.4 0.7 %copy.39.columns_ref = f32[64,5]{1,0:T(8,128)} copy(f32[64,5]{0,1:T(8,128)S(1)} %stack.23) | data formatting | bytes 2560 | tf_op jit(solution)/shard_map/stack | solution.py:441
  2.1 0.7 %copy.38.node_first_ref = bf16[128,64]{1,0:T(8,128)(2,1)} copy(bf16[128,64]{0,1:T(8,128)(2,1)S(1)} %copy-done.5) | data formatting | bytes 32768 | tf_op args[12]
  2.8 0.0 copy-done.2
  2.9 0.7 %copy.37.edge_first_ref = bf16[192,64]{1,0:T(8,128)(2,1)} copy(bf16[192,64]{0,1:T(8,128)(2,1)S(1)} %copy-done.2) | data formatting | bytes 49152 | tf_op args[7]
  3.6 9.5 %halo_out.1.ghost_ref = bf16[64,1536]{1,0:T(8,128)(2,1)} custom-call(bf16[64,1024]{1,0:T(8,128)(2,1)} %node_ref.3, s32[1,1536]{1,0:T(1,128)} %bitcast.20), custom_call_target="tpu_custom_call" | custom-call | tf_op jit(solution)/shard_map/halo_out/pallas_call | solution.py:427
  13.1 28.5 %local_layer.1 = (f32[64,1024]{1,0:T(8,128)}, bf16[12,64,128]{2,1,0:T(8,128)(2,1)}, bf16[64,3072]{1,0:T(8,128)(2,1)}, f32[256,128]{1,0:T(8,128)}) custom-call(bf16[64,1024]{1,0:T(8,128)(2,1)} %node_ref.3, bf16[64,1536]{1,0:T(8,128)(2,1)} %halo_out.1.ghost_ref, bf16[64,3072]{1,0:T(8,128)(2,1)} %edge_ref.1, s32[1,3072]{1,0:T(1,128)} %bitcast.22, ...), custom_call_target="tpu_custom_call" | custom-call | tf_op jit(solution)/shard_map/local_layer/pallas_call | solution.py:442
  41.6 20.1 %halo_back_and_sum.1 = (bf16[64,1024]{1,0:T(8,128)(2,1)}, f32[192,64]{1,0:T(8,128)}, f32[64,64]{1,0:T(8,128)}, f32[128,64]{1,0:T(8,128)}, f32[64,64]{1,0:T(8,128)}, /*index=5*/f32[8,64]{1,0:T(8,128)}) custom-call(bf16[12,64,128]{2,1,0:T(8,128)(2,1)} %get-tuple-element.22.ghost_ref, f32[64,1024]{1,0:T(8,128)} %get-tuple-element.23.local_ref, ...), custom_call_target="tpu_custom_call" | custom-call | tf_op jit(solution)/shard_map/halo_back_and_sum/pallas_call | solution.py:470
  61.7 1.4 %slice_bitcast_fusion = (f32[64]{0:T(128)}, f32[64]{0:T(128)}, f32[64]{0:T(128)}, f32[64]{0:T(128)}, f32[64]{0:T(128)}, /*index=5*/f32[64]{0:T(128)}) fusion(f32[8,64]{1,0:T(8,128)} %get-tuple-element.28), kind=kLoop, calls=%fused_computation | loop fusion | bytes 3072 | tf_op jit(solution)/shard_map/squeeze | solution.py:501
  63.2 1.6 %copy.41 = f32[128,64]{0,1:T(8,128)} copy(f32[128,64]{1,0:T(8,128)} %get-tuple-element.51) | data formatting | bytes 65536
  64.7 0.7 %copy.40 = f32[192,64]{0,1:T(8,128)} copy(f32[192,64]{1,0:T(8,128)S(1)} %copy-done.1) | data formatting | bytes 98304
  65.5 0.7 copy.45
  66.1 0.1 copy-done.4
  66.2 0.6 copy.46
  66.8 0.2 copy-done.3
  67.0 0.6 copy.47
  (11 shorter events, 0.0 us)
Async XLA Ops:
  0.6 0.7 copy-start.9
  0.7 0.7 copy-start.10
  0.7 0.7 copy-start.6
  0.7 0.7 copy-start.7
  0.7 0.7 %copy-start.8 = (f32[64]{0:T(128)S(1)}, f32[64]{0:T(128)}, u32[]{:S(2)}) copy-start(f32[64]{0:T(128)} %param.27) | copy-start | bytes 772
  1.4 0.7 %copy-start.5 = (bf16[128,64]{0,1:T(8,128)(2,1)S(1)}, bf16[128,64]{0,1:T(8,128)(2,1)}, u32[]{:S(2)}) copy-start(bf16[128,64]{0,1:T(8,128)(2,1)} %param.28) | copy-start | bytes 49156
  2.1 0.8 %copy-start.2 = (bf16[192,64]{0,1:T(8,128)(2,1)S(1)}, bf16[192,64]{0,1:T(8,128)(2,1)}, u32[]{:S(2)}) copy-start(bf16[192,64]{0,1:T(8,128)(2,1)} %param.23) | copy-start | bytes 73732
  61.7 3.0 %copy-start.1 = (f32[192,64]{1,0:T(8,128)S(1)}, f32[192,64]{1,0:T(8,128)}, u32[]{:S(2)}) copy-start(f32[192,64]{1,0:T(8,128)} %get-tuple-element.46) | copy-start | bytes 147460
  63.2 2.3 %copy-start = (bf16[64,1024]{1,0:T(8,128)(2,1)S(1)}, bf16[64,1024]{1,0:T(8,128)(2,1)}, u32[]{:S(2)}) copy-start(bf16[64,1024]{1,0:T(8,128)(2,1)} %get-tuple-element.74) | copy-start | bytes 393220
  65.5 0.8 %copy-start.4 = (f32[64,64]{1,0:T(8,128)S(1)}, f32[64,64]{1,0:T(8,128)}, u32[]{:S(2)}) copy-start(f32[64,64]{1,0:T(8,128)} %get-tuple-element.78) | copy-start | bytes 49156
  66.2 0.8 %copy-start.3 = (f32[64,64]{1,0:T(8,128)S(1)}, f32[64,64]{1,0:T(8,128)}, u32[]{:S(2)}) copy-start(f32[64,64]{1,0:T(8,128)} %get-tuple-element.83) | copy-start | bytes 49156

commit v2 on v1

v2 whole, which is shorter than its diff:
```python
import functools
import math

import jax
import jax.numpy as jnp
from jax import lax
from jax.experimental import pallas as pl
from jax.experimental.pallas import tpu as pltpu
from jax.sharding import PartitionSpec as P

EPSILON = 1e-05
MESH = pl.DeviceIdType.MESH
BF = jnp.bfloat16
F32 = jnp.float32


def nn(a, b):
    return lax.dot_general(a, b, (((1,), (0,)), ((), ())), preferred_element_type=F32)


def nt(a, b):
    return lax.dot_general(a, b, (((1,), (1,)), ((), ())), preferred_element_type=F32)


def flip(a):
    return a.astype(F32).T


def one_hot(index, rows):
    return jnp.where(lax.broadcasted_iota(jnp.int32, (rows, index.shape[1]), 0) == index, 1.0, 0.0).astype(BF)


def standardize(values):
    centered = values - jnp.mean(values, axis=0, keepdims=True)
    spread = lax.rsqrt(jnp.mean(centered * centered, axis=0, keepdims=True) + EPSILON)
    return centered * spread, spread


def normalize_back(upstream, scaled, spread, gain):
    weighted = upstream * gain
    return spread * (
        weighted
        - jnp.mean(weighted, axis=0, keepdims=True)
        - scaled * jnp.mean(weighted * scaled, axis=0, keepdims=True)
    )


def packed_rows(features):
    half = 3 * features // 2
    return half, half + features, half + 2 * features


def fold_lanes(values):
    total = values[:, :128]
    for begin in range(128, values.shape[1], 128):
        total = total + values[:, begin : begin + 128]
    return total


def halo_peers(dom, sub):
    d, s = lax.axis_index("dom"), lax.axis_index("sub")
    for o in (0, 2, 1):
        for r in range(sub):
            if o == 1 and r == 0:
                continue
            t = lax.rem(s + r, sub)
            target = d + (o - 1)
            yield o, t, target, (target >= 0) & (target < dom)


def halo_copy(outgoing, incoming, send_sem, recv_sem, source, landing, target, t):
    return pltpu.make_async_remote_copy(
        src_ref=outgoing.at[source],
        dst_ref=incoming.at[landing],
        send_sem=send_sem.at[source],
        recv_sem=recv_sem.at[landing],
        device_id=(target, t),
        device_id_type=MESH,
    )


def guarded(o, there, action):
    if o == 1:
        action()
    else:
        pl.when(there)(action)


def start_exchange(dom, sub, s, outgoing, incoming, send_sem, recv_sem, forward):
    for o, t, target, there in halo_peers(dom, sub):
        block = o if forward else 2 - o

        def start(block=block, t=t, target=target):
            halo_copy(outgoing, incoming, send_sem, recv_sem, block * sub + t, block * sub + s, target, t).start()

        guarded(o, there, start)
    d = lax.axis_index("dom")
    incoming[sub + s] = jnp.zeros(incoming.shape[1:], incoming.dtype)
    for o in (0, 2):
        origin = d + 1 - o if forward else d + o - 1

        @pl.when((origin < 0) | (origin >= dom))
        def _():
            for u in range(sub):
                incoming[o * sub + u] = jnp.zeros(incoming.shape[1:], incoming.dtype)


def finish_exchange(dom, sub, s, outgoing, incoming, send_sem, recv_sem, forward):
    for o, t, target, there in halo_peers(dom, sub):
        block = 2 - o if forward else o

        def finish(block=block, t=t, target=target):
            halo_copy(outgoing, incoming, send_sem, recv_sem, block * sub + t, block * sub + t, target, t).wait_recv()

        guarded(o, there, finish)
    for o, t, target, there in halo_peers(dom, sub):
        block = o if forward else 2 - o

        def finish(block=block, t=t, target=target):
            halo_copy(outgoing, incoming, send_sem, recv_sem, block * sub + t, block * sub + t, target, t).wait_send()

        guarded(o, there, finish)


def layer_kernel(
    dom, sub, chunk,
    node_ref, edge_ref, senders_ref, receivers_ref, index_ref, node_cot_ref, edge_cot_ref,
    edge_first_ref, edge_second_ref, node_first_ref, node_second_ref,
    edge_bias_ref, edge_gain_ref, edge_shift_ref, node_bias_ref, node_gain_ref,
    state_ref, edge_out_ref, sum_ref,
    outgoing, incoming, returning, returned, exports,
    selector, extended, slope, active, scaled_all, spread_all, summed, sums, small, lanes, local,
    packed_ref, pieces, reduced,
    send_sem, recv_sem, back_send, back_recv, part_send, part_recv, whole_send, whole_recv,
):
    features, cells = node_ref.shape
    faces = edge_ref.shape[1]
    peers, _, halo = outgoing.shape
    width = extended.shape[1]
    step = 128
    d, s = lax.axis_index("dom"), lax.axis_index("sub")
    count = dom * sub
    me = d * sub + s
    rows = reduced.shape[0]
    barrier = pltpu.get_barrier_semaphore()

    def place(r):
        other = lax.rem(me + r, count)
        return other, (other // sub, lax.rem(other, sub))

    def greet(r, carry):
        _, device = place(r)
        pl.semaphore_signal(barrier, inc=1, device_id=device, device_id_type=MESH)
        return carry

    lax.fori_loop(1, count, greet, 0)

    def pick(number, carry):
        chosen = index_ref[:, pl.ds(pl.multiple_of(number * 2 * halo, 2 * halo), 2 * halo)]
        exports[number] = one_hot(chosen, cells)
        picked = nn(node_ref[...], exports[number]).astype(BF)
        outgoing[2 * number] = picked[:, :halo]
        outgoing[2 * number + 1] = picked[:, halo:]
        return carry

    lax.fori_loop(0, peers // 2, pick, 0)
    pl.semaphore_wait(barrier, count - 1)
    start_exchange(dom, sub, s, outgoing, incoming, send_sem, recv_sem, forward=True)

    edge_first_t = edge_first_ref[...]
    edge_first = flip(edge_first_t).astype(BF)
    edge_second = edge_second_ref[...]
    edge_second_t = flip(edge_second).astype(BF)
    vectors = [edge_bias_ref, edge_gain_ref, edge_shift_ref, node_bias_ref, node_gain_ref]
    table = jnp.concatenate([v[...] for v in vectors] + [jnp.zeros((3, features), F32)], axis=0).T
    edge_bias, edge_gain, edge_shift, node_bias, node_gain = (table[:, i : i + 1] for i in range(5))
    summed[...] = jnp.zeros(summed.shape, F32)
    row = lax.broadcasted_iota(jnp.int32, (step, chunk), 0)

    def prepare(c, carry):
        here = pl.ds(pl.multiple_of(c * chunk, chunk), chunk)
        sender = senders_ref[:, here]
        receiver = receivers_ref[:, here]

        def fill(begin, index):
            def body(i, inner):
                at = pl.multiple_of(i * step, step)
                hit = row == (index - at)
                selector[c, pl.ds(pl.multiple_of(begin + at, step), step), :] = jnp.where(hit, 1.0, 0.0).astype(BF)
                return inner
            return body

        lax.fori_loop(0, width // step, fill(0, sender), 0)
        lax.fori_loop(0, cells // step, fill(width, receiver), 0)
        received = nn(node_ref[...], selector[c, width:, :]).astype(BF)
        stacked = jnp.concatenate([received, edge_ref[:, here]], axis=0)
        slope[:, here] = nn(edge_first_t[:, features:], stacked) + edge_bias
        return carry

    lax.fori_loop(0, faces // chunk, prepare, 0)
    finish_exchange(dom, sub, s, outgoing, incoming, send_sem, recv_sem, forward=True)
    extended[:, :cells] = node_ref[...]
    for k in range(peers):
        extended[:, cells + k * halo : cells + (k + 1) * halo] = incoming[k]

    def forward(c, carry):
        here = pl.ds(pl.multiple_of(c * chunk, chunk), chunk)
        sent = nn(extended[...], selector[c, :width, :]).astype(BF)
        linear = nn(edge_first_t[:, :features], sent) + slope[:, here]
        logistic = jax.nn.sigmoid(linear)
        lively = (linear * logistic).astype(BF)
        slope[:, here] = logistic * (1.0 + linear * (1.0 - logistic))
        active[:, here] = lively
        scaled, spread = standardize(nn(edge_second_t, lively))
        scaled_all[:, here] = scaled
        spread_all[:, here] = spread
        message = (scaled * edge_gain + edge_shift).astype(BF)
        summed[...] += nt(selector[c, width:, :], message)
        return carry

    lax.fori_loop(0, faces // chunk, forward, 0)

    node_first_t = node_first_ref[...]
    node_first = flip(node_first_t).astype(BF)
    node_second_t = flip(node_second_ref[...]).astype(BF)
    node_input = jnp.concatenate([node_ref[...], summed[...].T.astype(BF)], axis=0)
    node_linear = nn(node_first_t, node_input) + node_bias
    node_logistic = jax.nn.sigmoid(node_linear)
    node_active = (node_linear * node_logistic).astype(BF)
    node_scaled, node_spread = standardize(nn(node_second_t, node_active))
    upstream = node_cot_ref[...].astype(F32)
    lanes[3] = fold_lanes(upstream * node_scaled)
    lanes[4] = fold_lanes(upstream)
    node_delta = normalize_back(upstream, node_scaled, node_spread, node_gain).astype(BF)
    node_slope = node_logistic * (1.0 + node_linear * (1.0 - node_logistic))
    node_hidden = nn(node_second_ref[...], node_delta) * node_slope
    lanes[5] = fold_lanes(node_hidden)
    node_hidden = node_hidden.astype(BF)
    node_first_delta = nt(node_input, node_hidden)
    half, mid, top = packed_rows(features)
    packed_ref[half:mid, :features] = node_first_delta[:features]
    packed_ref[half:mid, features:] = node_first_delta[features:]
    packed_ref[mid:top, features:] = nt(node_active, node_delta)
    node_back = nn(node_first, node_hidden)
    local[...] = node_back[:features] + upstream
    toward = node_back[features:]
    high = toward.astype(BF)
    low = (toward - high.astype(F32)).astype(BF)
    toward = jnp.concatenate([high, low], axis=0)

    sums[...] = jnp.zeros(sums.shape, F32)
    small[...] = jnp.zeros(small.shape, F32)
    for i in range(3):
        lanes[i] = jnp.zeros(lanes.shape[1:], F32)

    def backward(c, carry):
        here = pl.ds(pl.multiple_of(c * chunk, chunk), chunk)
        gathered = nn(toward, selector[c, width:, :])
        cotangent = edge_cot_ref[:, here].astype(F32)
        delta = cotangent + (gathered[:features] + gathered[features:])
        scaled = scaled_all[:, here]
        lanes[0] += fold_lanes(delta * scaled)
        lanes[1] += fold_lanes(delta)
        edge_delta = normalize_back(delta, scaled, spread_all[:, here], edge_gain).astype(BF)
        small[0] += nt(active[:, here], edge_delta)
        hidden = nn(edge_second, edge_delta) * slope[:, here]
        lanes[2] += fold_lanes(hidden)
        hidden = hidden.astype(BF)
        active[:, here] = hidden
        small[1] += nt(edge_ref[:, here], hidden)
        sums[...] += nt(selector[c], hidden)
        return carry

    lax.fori_loop(0, faces // chunk, backward, 0)

    by_sender = sums[:width, :].astype(BF)
    by_receiver = sums[width:, :].astype(BF)
    back = nt(edge_first[:features], by_sender)
    for k in range(peers):
        returning[k] = back[:, cells + k * halo : cells + (k + 1) * halo].astype(BF)
    first = nn(extended[...], by_sender)
    second = nn(node_ref[...], by_receiver)
    packed_ref[0:features, :features] = first
    packed_ref[features:half, :features] = second[: half - features]
    packed_ref[0 : 2 * features - half, features:] = second[half - features :]
    packed_ref[2 * features - half : half, features:] = small[1]
    packed_ref[mid:top, :features] = small[0]
    column = lax.broadcasted_iota(jnp.int32, (features, 128), 1)
    vectors = jnp.zeros((features, 128), F32)
    for i in range(6):
        vectors = jnp.where(column == i, jnp.sum(lanes[i], axis=1, keepdims=True), vectors)
    packed_ref[top:, :] = jnp.zeros((packed_ref.shape[0] - top, 128), F32)
    packed_ref[top : top + 8, :features] = vectors.T[:8]

    def part_copy(source, landing, device):
        return pltpu.make_async_remote_copy(
            src_ref=packed_ref.at[pl.ds(pl.multiple_of(source * rows, 8), rows)],
            dst_ref=pieces.at[landing],
            send_sem=part_send.at[source],
            recv_sem=part_recv.at[landing],
            device_id=device,
            device_id_type=MESH,
        )

    def whole_copy(landing, device, other):
        return pltpu.make_async_remote_copy(
            src_ref=reduced,
            dst_ref=sum_ref.at[pl.ds(pl.multiple_of(landing * rows, 8), rows)],
            send_sem=whole_send.at[other],
            recv_sem=whole_recv.at[landing],
            device_id=device,
            device_id_type=MESH,
        )

    def send_part(r, carry):
        other, device = place(r)
        part_copy(other, me, device).start()
        return carry

    lax.fori_loop(1, count, send_part, 0)
    start_exchange(dom, sub, s, returning, returned, back_send, back_recv, forward=False)
    local[...] += back[:, :cells] + nt(edge_first[features : 2 * features], by_receiver)

    def emit(c, carry):
        here = pl.ds(pl.multiple_of(c * chunk, chunk), chunk)
        ahead = nn(edge_first[2 * features :], active[:, here])
        edge_out_ref[:, here] = (edge_cot_ref[:, here].astype(F32) + ahead).astype(BF)
        return carry

    lax.fori_loop(0, faces // chunk, emit, 0)
    own = pl.ds(pl.multiple_of(me * rows, 8), rows)

    def take_part(r, total):
        other, device = place(r)
        part_copy(other, other, device).wait_recv()
        return total + pieces[other]

    reduced[...] = lax.fori_loop(1, count, take_part, packed_ref[own, :])

    def send_whole(r, carry):
        other, device = place(r)
        whole_copy(me, device, other).start()
        return carry

    lax.fori_loop(1, count, send_whole, 0)
    sum_ref[own, :] = reduced[...]
    finish_exchange(dom, sub, s, returning, returned, back_send, back_recv, forward=False)
    summed[...] = jnp.zeros(summed.shape, F32)

    def scatter(i, carry):
        value = jnp.concatenate([returned[2 * i], returned[2 * i + 1]], axis=1)
        summed[...] += nt(exports[i], value)
        return carry

    lax.fori_loop(0, peers // 2, scatter, 0)
    state_ref[...] = (local[...] + summed[...].T).astype(BF)

    def settle(r, carry):
        other, device = place(r)
        part_copy(other, other, device).wait_send()
        whole_copy(other, device, other).wait_send()
        whole_copy(other, device, other).wait_recv()
        return carry

    lax.fori_loop(1, count, settle, 0)


def unpack_kernel(
    factor, state_in, edge_in, sum_ref,
    state_ref, edge_ref, edge_first_ref, edge_second_ref, node_first_ref, node_second_ref, *vector_refs,
):
    features = state_in.shape[0]
    half, mid, top = packed_rows(features)
    state_ref[...] = state_in[...]
    edge_ref[...] = edge_in[...]
    left = sum_ref[:, :features] * factor
    right = sum_ref[:, features:] * factor
    edge_first_ref[...] = jnp.concatenate([left[:half], right[:half]], axis=0).T
    node_first_ref[...] = jnp.concatenate([left[half:mid], right[half:mid]], axis=0).T
    edge_second_ref[...] = left[mid:top]
    node_second_ref[...] = right[mid:top]
    for i, vector_ref in enumerate(vector_refs):
        vector_ref[...] = left[top + i : top + i + 1]


def on_device(
    dom, sub,
    node_state, edge_state, senders, receivers, send_index, node_cotangent, edge_cotangent,
    edge_first, edge_bias, edge_second, edge_gain, edge_shift, node_first, node_bias, node_second, node_gain,
):
    features, cells = node_state.shape
    faces = edge_state.shape[1]
    halo = send_index.shape[2]
    peers = 3 * sub
    ghosts = peers * halo
    width = cells + ghosts
    count = dom * sub
    rows = -(-(packed_rows(features)[2] + 8) // (8 * count)) * 8
    chunk = math.gcd(faces, 512)
    vmem = pl.BlockSpec(memory_space=pltpu.VMEM)
    shape = jax.ShapeDtypeStruct
    dma = pltpu.SemaphoreType.DMA

    def line(vector):
        return vector.reshape(1, -1)

    state, edge_result, total = pl.pallas_call(
        functools.partial(layer_kernel, dom, sub, chunk),
        out_shape=(
            shape((features, cells), BF),
            shape((features, faces), BF),
            shape((count * rows, 128), F32),
        ),
        in_specs=[vmem] * 16,
        out_specs=(vmem,) * 3,
        scratch_shapes=[pltpu.VMEM((peers, features, halo), BF)] * 4
        + [
            pltpu.VMEM((peers // 2, cells, 2 * halo), BF),
            pltpu.VMEM((faces // chunk, width + cells, chunk), BF),
            pltpu.VMEM((features, width), BF),
            pltpu.VMEM((features, faces), F32),
            pltpu.VMEM((features, faces), BF),
            pltpu.VMEM((features, faces), F32),
            pltpu.VMEM((1, faces), F32),
            pltpu.VMEM((cells, features), F32),
            pltpu.VMEM((width + cells, features), F32),
            pltpu.VMEM((2, features, features), F32),
            pltpu.VMEM((6, features, 128), F32),
            pltpu.VMEM((features, cells), F32),
            pltpu.VMEM((count * rows, 128), F32),
            pltpu.VMEM((count, rows, 128), F32),
            pltpu.VMEM((rows, 128), F32),
        ]
        + [dma((peers,))] * 4
        + [dma((count,))] * 4,
        compiler_params=pltpu.CompilerParams(
            collective_id=0, has_side_effects=True, vmem_limit_bytes=60 * 1024 * 1024
        ),
        name="layer",
    )(
        node_state, edge_state, line(senders), line(receivers), line(send_index),
        node_cotangent, edge_cotangent, edge_first.T, edge_second, node_first.T, node_second,
        line(edge_bias), line(edge_gain), line(edge_shift), line(node_bias), line(node_gain),
    )
    vector = shape((1, features), F32)
    state, edge_result, edge_first_sum, edge_second_sum, node_first_sum, node_second_sum, *vectors = pl.pallas_call(
        functools.partial(unpack_kernel, 1.0 / math.sqrt(faces * count)),
        out_shape=(
            shape((features, cells), BF),
            shape((features, faces), BF),
            shape(edge_first.shape[::-1], F32),
            shape(edge_second.shape, F32),
            shape(node_first.shape[::-1], F32),
            shape(node_second.shape, F32),
        )
        + (vector,) * 6,
        in_specs=[vmem] * 3,
        out_specs=(vmem,) * 12,
        name="unpack",
    )(state, edge_result, total)
    vectors = [v.reshape(-1) for v in vectors]
    return (
        state, edge_result, edge_first_sum.T, vectors[2], edge_second_sum, vectors[0], vectors[1],
        node_first_sum.T, vectors[5], node_second_sum, vectors[3], vectors[4],
    )


def solution(mesh):
    split = P(None, ("dom", "sub"))
    faces = P(("dom", "sub"))
    return jax.shard_map(
        functools.partial(on_device, mesh.shape["dom"], mesh.shape["sub"]),
        mesh=mesh,
        in_specs=(split, split, faces, faces, P(("dom", "sub"), None, None), split, split) + (P(),) * 9,
        out_specs=(split, split) + (P(),) * 10,
        check_vma=False,
    )
```

time: 68.1 us -> 52.2 us (0.77)
  local copies, waits for them, and re-layouts: 8.76 us -> 0 us
  Pallas kernels: 58.1 us -> 51.3 us
    pallas_call x3 -> x2, Pallas kernels: 58.1 us -> 51.3 us  [the longest x1 49.3 us: on_device(): pl.pallas_call(functools.partial(layer_kernel, dom, sub, chunk), out_shap...]
    unnamed x29 -> x0, local copies, waits for them, and re-layouts: 6.59 us -> none
    squeeze x1 -> x0, local copies, waits for them, and re-layouts: 1.43 us -> none  [on_device(): vectors[4]]
    another operation x2 -> x0, local copies, waits for them, and re-layouts: 0.73 us -> none  [on_device(): jnp.stack([edge_bias, edge_gain, edge_shift, node_bias, node_gain], axis=1)]
where the time goes in v2:
time: 52.2 us; the launch traced here: 52 us
  Pallas kernels  51.3 us (98%)
  between operations  0.66 us (1%)
    pallas_call x1, Pallas kernels, on_device(): pl.pallas_call(functools.partial(layer_kernel, dom, sub, chunk), out_shap...  49.3 us
    pallas_call x1, Pallas kernels, on_device(): pl.pallas_call(functools.partial(unpack_kernel, 1.0 / math.sqrt(faces * c...  2.09 us

profile of v2, /device:TPU:0, one launch (start us, length us, event | category | flops | bytes accessed | tf_op | source)
XLA Modules:
  0.0 52.0 jit_solution(13710442152981682609)
XLA Ops:
  0.7 49.3 %layer.1 = (bf16[64,1024]{1,0:T(8,128)(2,1)}, bf16[64,3072]{1,0:T(8,128)(2,1)}, f32[256,128]{1,0:T(8,128)}) custom-call(bf16[64,1024]{1,0:T(8,128)(2,1)} %node_ref.1, bf16[64,3072]{1,0:T(8,128)(2,1)} %edge_ref.1, s32[1,3072]{1,0:T(1,128)} %bitcast.20, s32[1,3072]{1,0:T(1,128)} %bitcast.21, s32[1,1536]{1,0:T(1,128)} %bitcast.22, ...), custom_call_target="tpu_custom_call" | custom-call | tf_op jit(solution)/shard_map/layer/pallas_call | solution.py:407
  49.9 2.1 %unpack.1 = (bf16[64,1024]{1,0:T(8,128)(2,1)}, bf16[64,3072]{1,0:T(8,128)(2,1)}, f32[64,192]{1,0:T(8,128)}, f32[64,64]{1,0:T(8,128)}, f32[64,128]{1,0:T(8,128)},...) custom-call(bf16[64,1024]{1,0:T(8,128)(2,1)} %get-tuple-element.27.s, ...), custom_call_target="tpu_custom_call" | custom-call | tf_op jit(solution)/shard_map/unpack/pallas_call | solution.py:446

commit v3 on v2

--- a/solution.py
+++ b/solution.py
@@ -176,6 +176,7 @@
     edge_bias, edge_gain, edge_shift, node_bias, node_gain = (table[:, i : i + 1] for i in range(5))
     summed[...] = jnp.zeros(summed.shape, F32)
     row = lax.broadcasted_iota(jnp.int32, (step, chunk), 0)
+    one, zero = jnp.ones((step, chunk), BF), jnp.zeros((step, chunk), BF)
 
     def prepare(c, carry):
         here = pl.ds(pl.multiple_of(c * chunk, chunk), chunk)
@@ -183,10 +184,12 @@
         receiver = receivers_ref[:, here]
 
         def fill(begin, index):
+            offset = (jnp.broadcast_to(index, (step, chunk)) - row).astype(jnp.int16)
+
             def body(i, inner):
                 at = pl.multiple_of(i * step, step)
-                hit = row == (index - at)
-                selector[c, pl.ds(pl.multiple_of(begin + at, step), step), :] = jnp.where(hit, 1.0, 0.0).astype(BF)
+                hit = offset == jnp.full((step, chunk), at, jnp.int32).astype(jnp.int16)
+                selector[c, pl.ds(pl.multiple_of(begin + at, step), step), :] = jnp.where(hit, one, zero)
                 return inner
             return body
 
@@ -248,7 +251,6 @@
     low = (toward - high.astype(F32)).astype(BF)
     toward = jnp.concatenate([high, low], axis=0)
 
-    sums[...] = jnp.zeros(sums.shape, F32)
     small[...] = jnp.zeros(small.shape, F32)
     for i in range(3):
         lanes[i] = jnp.zeros(lanes.shape[1:], F32)
@@ -268,10 +270,20 @@
         hidden = hidden.astype(BF)
         active[:, here] = hidden
         small[1] += nt(edge_ref[:, here], hidden)
-        sums[...] += nt(selector[c], hidden)
         return carry
 
     lax.fori_loop(0, faces // chunk, backward, 0)
+    block = math.gcd(width + cells, 512)
+
+    def gather_sums(i, carry):
+        at = pl.ds(pl.multiple_of(i * block, block), block)
+        total = nt(selector[0, at, :], active[:, :chunk])
+        for c in range(1, faces // chunk):
+            total = total + nt(selector[c, at, :], active[:, c * chunk : (c + 1) * chunk])
+        sums[at, :] = total
+        return carry
+
+    lax.fori_loop(0, (width + cells) // block, gather_sums, 0)
 
     by_sender = sums[:width, :].astype(BF)
     by_receiver = sums[width:, :].astype(BF)

time: 52.2 us -> 51.7 us (level)
  no operation moved by 1% of the time
where the time goes in v3:
time: 51.7 us; the launch traced here: 51.5 us
  Pallas kernels  50.9 us (98%)
  between operations  0.66 us (1%)
    pallas_call x1, Pallas kernels, on_device(): pl.pallas_call(functools.partial(layer_kernel, dom, sub, chunk), out_shap...  48.8 us
    pallas_call x1, Pallas kernels, on_device(): pl.pallas_call(functools.partial(unpack_kernel, 1.0 / math.sqrt(faces * c...  2.09 us

profile of v3, /device:TPU:0, one launch (start us, length us, event | category | flops | bytes accessed | tf_op | source)
XLA Modules:
  0.0 51.5 jit_solution(3085338478857963652)
XLA Ops:
  0.7 48.8 %layer.1 = (bf16[64,1024]{1,0:T(8,128)(2,1)}, bf16[64,3072]{1,0:T(8,128)(2,1)}, f32[256,128]{1,0:T(8,128)}) custom-call(bf16[64,1024]{1,0:T(8,128)(2,1)} %node_ref.1, bf16[64,3072]{1,0:T(8,128)(2,1)} %edge_ref.1, s32[1,3072]{1,0:T(1,128)} %bitcast.20, s32[1,3072]{1,0:T(1,128)} %bitcast.21, s32[1,1536]{1,0:T(1,128)} %bitcast.22, ...), custom_call_target="tpu_custom_call" | custom-call | tf_op jit(solution)/shard_map/layer/pallas_call | solution.py:419
  49.4 2.1 %unpack.1 = (bf16[64,1024]{1,0:T(8,128)(2,1)}, bf16[64,3072]{1,0:T(8,128)(2,1)}, f32[64,192]{1,0:T(8,128)}, f32[64,64]{1,0:T(8,128)}, f32[64,128]{1,0:T(8,128)},...) custom-call(bf16[64,1024]{1,0:T(8,128)(2,1)} %get-tuple-element.27.s, ...), custom_call_target="tpu_custom_call" | custom-call | tf_op jit(solution)/shard_map/unpack/pallas_call | solution.py:458
